TPU v7x, 32 devices: a whole 2x2x4 slice. The times are simulated.
32 devices in a mesh: heads: 4 (over y, core), tokens: 4 (over z), cols: 2 (over x).
Axes of the slice: x: 2, y: 2, z: 4, core: 2. Of those that a mesh axis runs over, the one named last changes fastest.
Arguments:
- query_in: bfloat16 [2048, 8192], P('tokens', ('heads', 'cols')), may hold values from -24 to 24
- key_in: bfloat16 [2048, 8192], P('tokens', ('heads', 'cols')), may hold values from -24 to 24
- value_in: bfloat16 [2048, 8192], P('tokens', ('heads', 'cols')), may hold values from -6 to 6
- out_grads: bfloat16 [2048, 8192], P('tokens', ('heads', 'cols')), may hold values from -6 to 6
- doc_starts: int32 [6], replicated, may hold values from 0 to 2047, as said below
Outputs:
- input_factor: float32 [8192, 8192], P('heads', ('tokens', 'cols'))
- grad_factor: float32 [8192, 8192], P('heads', ('tokens', 'cols'))
Inputs may be any that keep to these rules, and one draw needn't show every extreme that they name: Strictly increasing with the first entry 0; document d runs from doc_starts[d] to the next start (the last one to 2048) - 1. One document holds (4 // 2 + 1) * 512 tokens.
All inputs are finite; a program needn't handle non-finite values.
Results may differ from a plain program's by a relative error of at most 0.0041.
Values may be sent and summed in bfloat16 or wider, within the bound.
A program may use at most 128 MiB of HBM per device.

v0:
```python
import math
import jax
import jax.numpy as jnp
from jax import lax
from jax.sharding import PartitionSpec as P

HEAD_DIM = 128
MASK_FLOOR = -1e30


def spread(value, axis, source):
    kept = jnp.where(lax.axis_index(axis) == source, value, 0).astype(value.dtype)
    return lax.psum(kept, axis)


def document_ids(positions, doc_starts):
    return jnp.sum((positions[:, None] >= doc_starts[None, :]).astype(jnp.int32), axis=1) - 1


def pair_scores(query_rows, key_rows, query_pos, key_pos, doc_starts):
    head_count = query_rows.shape[1] // HEAD_DIM
    query_heads = query_rows.reshape(query_rows.shape[0], head_count, HEAD_DIM)
    key_heads = key_rows.reshape(key_rows.shape[0], head_count, HEAD_DIM)
    scores = jnp.einsum(
        "qhd,khd->hqk", query_heads, key_heads, preferred_element_type=jnp.float32
    ) * (1.0 / math.sqrt(HEAD_DIM))
    query_docs = document_ids(query_pos, doc_starts)
    key_docs = document_ids(key_pos, doc_starts)
    allowed = query_docs[:, None] == key_docs[None, :]
    return (scores, allowed[None, :, :])


def on_device(query_in, key_in, value_in, out_grads, doc_starts):
    tok_dev, row_width = query_in.shape
    head_count = row_width // HEAD_DIM
    first_pos = lax.axis_index("tokens") * tok_dev
    query_pos = first_pos + jnp.arange(tok_dev, dtype=jnp.int32)
    keys_all, values_all = (
        lax.all_gather(key_in, "tokens", axis=0, tiled=True),
        lax.all_gather(value_in, "tokens", axis=0, tiled=True),
    )
    all_tokens = keys_all.shape[0]
    key_span = min(512, all_tokens)
    block_ids = jnp.arange(all_tokens // key_span, dtype=jnp.int32)

    def block_scores(block_id):
        key_begin = block_id * key_span
        key_rows = lax.dynamic_slice_in_dim(keys_all, key_begin, key_span, 0)
        key_pos = key_begin + jnp.arange(key_span, dtype=jnp.int32)
        scores, allowed = pair_scores(query_in, key_rows, query_pos, key_pos, doc_starts)
        return (key_begin, scores, allowed)

    def gated(block_id, update, running):
        key_begin = block_id * key_span
        return update(running)

    def stats_step(running, block_id):

        def update(state):
            row_peak, row_mass = state
            key_begin, scores, allowed = block_scores(block_id)
            masked = jnp.where(allowed, scores, MASK_FLOOR)
            new_peak = jnp.maximum(row_peak, jnp.max(masked, axis=2))
            new_mass = row_mass * jnp.exp(row_peak - new_peak) + jnp.sum(
                jnp.where(allowed, jnp.exp(masked - new_peak[:, :, None]), 0.0), axis=2
            )
            return (new_peak, new_mass)

        return (gated(block_id, update, running), None)

    initial = (
        jnp.full((head_count, tok_dev), MASK_FLOOR, jnp.float32),
        jnp.zeros((head_count, tok_dev), jnp.float32),
    )
    (row_peak, row_mass), _ = lax.scan(stats_step, initial, block_ids)
    log_total = row_peak + jnp.log(row_mass)

    def value_step(running, block_id):

        def update(state):
            weighted, partials = state
            key_begin, scores, allowed = block_scores(block_id)
            weights = jnp.where(allowed, jnp.exp(scores - log_total[:, :, None]), 0.0).astype(
                jnp.bfloat16
            )
            value_rows = lax.dynamic_slice_in_dim(values_all, key_begin, key_span, 0).reshape(
                key_span, head_count, HEAD_DIM
            )
            weighted = weighted + jnp.einsum(
                "hqk,khd->qhd", weights, value_rows, preferred_element_type=jnp.float32
            )
            return (weighted, partials)

        return (gated(block_id, update, running), None)

    partial_rows = 8
    value_init = (
        jnp.zeros((tok_dev, head_count, HEAD_DIM), jnp.float32),
        jnp.zeros((partial_rows, row_width), jnp.float32),
    )
    (weighted, partials), _ = lax.scan(value_step, value_init, block_ids)
    attended = weighted.reshape(tok_dev, row_width).astype(jnp.bfloat16)
    stats_all = lax.all_gather(log_total.T, "tokens", axis=0, tiled=True)
    query_rows = lax.all_gather(query_in, "tokens", axis=0, tiled=True)
    grad_rows = lax.all_gather(out_grads, "tokens", axis=0, tiled=True)
    piece_rows = query_rows.shape[0]
    piece_pos = jnp.arange(piece_rows, dtype=jnp.int32)

    def update(grad_sum):
        scores, allowed = pair_scores(query_rows, key_in, piece_pos, query_pos, doc_starts)
        weights = jnp.where(allowed, jnp.exp(scores - stats_all.T[:, :, None]), 0.0).astype(
            jnp.bfloat16
        )
        piece_grads = grad_rows.reshape(piece_rows, head_count, HEAD_DIM)
        return jnp.einsum("hqk,qhd->khd", weights, piece_grads, preferred_element_type=jnp.float32)

    summed = update(jnp.zeros((tok_dev, head_count, HEAD_DIM), jnp.float32))
    value_grads = summed.reshape(tok_dev, row_width).astype(jnp.bfloat16)
    token_shards = lax.axis_size("tokens")
    col_shards = lax.axis_size("cols")
    rows_attended, rows_grads = (
        lax.all_gather(attended[None], ("tokens", "cols"), axis=0, tiled=True),
        lax.all_gather(value_grads[None], ("tokens", "cols"), axis=0, tiled=True),
    )
    rows_attended = rows_attended.reshape(token_shards, col_shards, tok_dev, row_width)
    rows_grads = rows_grads.reshape(token_shards, col_shards, tok_dev, row_width)
    own_attended = lax.dynamic_index_in_dim(
        rows_attended, lax.axis_index("cols"), 1, keepdims=False
    )
    own_grads = lax.dynamic_index_in_dim(rows_grads, lax.axis_index("cols"), 1, keepdims=False)
    cols_attended, cols_grads = (
        spread(own_attended, "heads", lax.axis_index("tokens")),
        spread(own_grads, "heads", lax.axis_index("tokens")),
    )
    input_factor = jnp.einsum(
        "acnf,ang->cfg", rows_attended, cols_attended, preferred_element_type=jnp.float32
    )
    grad_factor = jnp.einsum(
        "acnf,ang->cfg", rows_grads, cols_grads, preferred_element_type=jnp.float32
    )
    input_factor = input_factor.reshape(col_shards * row_width, row_width) / all_tokens
    grad_factor = grad_factor.reshape(col_shards * row_width, row_width) / all_tokens
    return (input_factor, grad_factor)


def solution(mesh):
    in_specs = (
        P("tokens", ("heads", "cols")),
        P("tokens", ("heads", "cols")),
        P("tokens", ("heads", "cols")),
        P("tokens", ("heads", "cols")),
        P(),
    )
    out_specs = (P("heads", ("tokens", "cols")), P("heads", ("tokens", "cols")))
    return jax.shard_map(
        on_device, mesh=mesh, in_specs=in_specs, out_specs=out_specs, check_vma=False
    )
```

profile of v0, /device:TPU:0, one launch (start us, length us, event | category | flops | bytes accessed | tf_op | source)
XLA Modules:
  0.0 775.8 jit_solution(3249628128545039161)
XLA Ops:
  7.2 2.4 copy.58
  9.7 2.3 copy.57
  12.0 0.7 all-gather.15.cloned.1.call-update
  12.8 2.3 copy.62
  15.1 78.1 %all-gather.9.cloned.1.call-done = bf16[2048,1024]{0,1:T(8,128)(2,1)} async-done(((bf16[512,1024]{0,1:T(8,128)(2,1)}), bf16[2048,1024]{0,1:T(8,128)(2,1)}) %all-gather.9.cloned.1.call-update) | async-done | bytes 4194320 | tf_op jit(solution)/shard_map/all_gather | solution.py:39
  93.2 27.0 %while.30 = (s32[]{:T(128)}, f32[8,512]{1,0:T(8,128)S(1)}, f32[8,512]{1,0:T(8,128)S(1)}, s32[6]{0:T(128)S(1)}, s32[4]{0:T(128)S(1)}, /*index=5*/bf16[2048,1024]{...) while((s32[]{:T(128)}, f32[8,512]{1,0:T(8,128)S(1)}, ...), condition=%wide.region_5.6_spmd.clone, body=%wide.region_0.5_spmd.clone.sunk | while | flops 553950208 | bytes 21995748 | solution.py:75
  93.2 0.6 dynamic_slice.60
  94.6 0.2 broadcast_compare_fusion.5
  94.8 1.3 constant_dynamic-slice_fusion.5
  96.1 1.7 fusion.59
  97.9 2.0 select_reduce_fusion.2
  100.0 0.6 dynamic_slice.60
  101.3 0.2 broadcast_compare_fusion.5
  101.5 1.4 constant_dynamic-slice_fusion.5
  102.9 1.7 fusion.59
  104.7 2.0 select_reduce_fusion.2
  106.8 0.6 dynamic_slice.60
  108.2 0.2 broadcast_compare_fusion.5
  108.4 1.3 constant_dynamic-slice_fusion.5
  109.7 1.7 fusion.59
  111.4 2.0 select_reduce_fusion.2
  113.5 0.6 dynamic_slice.60
  114.9 0.2 broadcast_compare_fusion.5
  115.1 1.3 constant_dynamic-slice_fusion.5
  116.4 1.7 fusion.59
  118.2 2.0 select_reduce_fusion.2
  120.3 54.3 %all-gather.7.cloned.1.call-done = bf16[2048,1024]{0,1:T(8,128)(2,1)} async-done(((bf16[512,1024]{0,1:T(8,128)(2,1)}), bf16[2048,1024]{0,1:T(8,128)(2,1)}) %all-gather.7.cloned.1.call-update) | async-done | bytes 4194320 | tf_op jit(solution)/shard_map/all_gather | solution.py:40
  174.6 34.2 %while.31 = (s32[]{:T(128)}, f32[512,8,128]{0,2,1:T(8,128)}, s32[4]{0:T(128)S(1)}, bf16[2048,1024]{0,1:T(8,128)(2,1)}, s32[6]{0:T(128)S(1)}, /*index=5*/bf16[204...) while((s32[]{:T(128)}, f32[512,8,128]{0,2,1:T(8,128)}, ...), condition=%wide.region_9.10_spmd.clone, body=%wide.region_6.9_spmd.clone.sunk | while | flops 1083460608 | bytes 12099821 | solution.py:101
  174.6 0.6 dynamic_slice.62
  176.0 0.2 broadcast_compare_fusion.6
  176.2 1.7 constant_dynamic-slice_fusion.6
  177.9 4.0 bitcast_add_fusion.2
  181.9 0.6 dynamic_slice.62
  183.3 0.2 broadcast_compare_fusion.6
  183.5 1.9 constant_dynamic-slice_fusion.6
  185.4 5.6 bitcast_add_fusion.2
  191.0 0.6 dynamic_slice.62
  192.4 0.2 broadcast_compare_fusion.6
  192.6 1.7 constant_dynamic-slice_fusion.6
  194.3 5.6 bitcast_add_fusion.2
  199.9 0.6 dynamic_slice.62
  201.3 0.2 broadcast_compare_fusion.6
  201.5 1.7 constant_dynamic-slice_fusion.6
  203.2 5.6 bitcast_add_fusion.2
  208.8 1.8 convert_element_type.76
  210.7 1.3 copy.73
  212.1 0.1 convert_reduce_fusion.4
  212.3 0.8 broadcast_compare_fusion.2
  213.0 42.4 %all-gather.15.cloned.1.call-done = bf16[2048,1024]{1,0:T(8,128)(2,1)} async-done(((bf16[512,1024]{1,0:T(8,128)(2,1)}), bf16[2048,1024]{1,0:T(8,128)(2,1)}) %all-gather.15.cloned.1.call-update) | async-done | bytes 4194320 | tf_op jit(solution)/shard_map/all_gather | solution.py:105
  255.5 6.4 copy.65
  261.9 15.2 %all_gather.25 = f32[2048,8]{0,1:T(8,128)S(1)} all-gather(f32[512,8]{0,1:T(8,128)S(1)} %bitcast.132), channel_id=1, replica_groups=mesh['heads'=4,'tokens'=4,'cols'=2] {'tokens'}, dimensions={0}, use_global_device_ids=true | all-gather | bytes 81920 | tf_op jit(solution)/shard_map/all_gather | solution.py:103
  277.1 59.8 %all-gather.13.cloned.1.call-done = bf16[2048,1024]{0,1:T(8,128)(2,1)} async-done(((bf16[512,1024]{0,1:T(8,128)(2,1)}), bf16[2048,1024]{0,1:T(8,128)(2,1)}) %all-gather.13.cloned.1.call-update) | async-done | bytes 4194320 | tf_op jit(solution)/shard_map/all_gather | solution.py:104
  336.9 14.4 %fusion.29 = bf16[8,512,128]{1,2,0:T(8,128)(2,1)S(1)} fusion(bf16[2048,8,128]{0,2,1:T(8,128)(2,1)} %bitcast.130, bf16[2048,8,128]{0,2,1:T(8,128)(2,1)} %bitcast.134, f32[8,2048]{1,0:T(8,128)S(1)} %bitcast.133, pred[2048,512]{1,0:T(8,128)(4,1)S(1)} %broadcast_compare_fusion.2, bf16[512,1024]{1,0:T(8,128)(2,1)S(1)} %copy-done.2), kind=kOutput, calls=%fused_computation.50 | convolution fusion | flops 4329046016 | bytes 11599872 | tf_op jit(solution)/shard_map/hqk,qhd->khd/dot_general | solution.py:115
  351.3 1.3 copy.66
  352.7 0.3 all-reduce.3.cloned.1.call-start
  353.0 109.4 %all-gather.11.cloned.1.call-done = bf16[8,512,1024]{2,1,0:T(8,128)(2,1)} async-done(((bf16[1,512,1024]{2,1,0:T(8,128)(2,1)}), bf16[8,512,1024]{2,1,0:T(8,128)(2,1)}) %all-gather.11.cloned.1.call-update) | async-done | bytes 8388624 | tf_op jit(solution)/shard_map/all_gather | solution.py:122
  462.4 4.5 fusion.27
  466.9 120.8 %all-gather.17.cloned.1.call-done = bf16[8,512,1024]{2,1,0:T(8,128)(2,1)} async-done(((bf16[1,512,1024]{2,1,0:T(8,128)(2,1)}), bf16[8,512,1024]{2,1,0:T(8,128)(2,1)}) %all-gather.17.cloned.1.call-update) | async-done | bytes 8388624 | tf_op jit(solution)/shard_map/all_gather | solution.py:123
  587.6 4.4 fusion.26
  592.1 11.5 %copy.60 = bf16[2,1024,4,512]{3,1,0,2:T(8,128)(2,1)} copy(bf16[2,1024,4,512]{1,3,0,2:T(8,128)(2,1)} %bitcast.124) | data formatting | bytes 16777216 | tf_op jit(solution)/shard_map/acnf,ang->cfg/dot_general | solution.py:135
  603.6 11.5 %copy.67 = bf16[2,1024,4,512]{3,1,0,2:T(8,128)(2,1)} copy(bf16[2,1024,4,512]{1,3,0,2:T(8,128)(2,1)} %bitcast.126) | data formatting | bytes 16777216 | tf_op jit(solution)/shard_map/acnf,ang->cfg/dot_general | solution.py:138
  615.1 128.2 %all-reduce.3.cloned.1.call-done = (bf16[4,512,1024]{2,1,0:T(8,128)(2,1)}, bf16[4,512,1024]{2,1,0:T(8,128)(2,1)}) async-done(((bf16[4,512,1024]{2,1,0:T(8,128)(2,1)}, bf16[4,512,1024]{2,1,0:T(8,128)(2,1)}), (bf16[4,512,1024]{2,1,0:T(8,128)(2,1)}, bf16[4,512,1024]{2,1,0:T(8,128)(2,1)})) %all-reduce.3.cloned.1.call-update) | async-done | bytes 8388624 | tf_op jit(solution)/shard_map/psum | solution.py:13
  743.3 14.6 %bitcast_multiply_fusion.1 = f32[2048,1024]{1,0:T(8,128)} fusion(bf16[2048,4,512]{2,0,1:T(8,128)(2,1)} %bitcast.128, bf16[4,512,1024]{2,1,0:T(8,128)(2,1)} %get-tuple-element.383), kind=kOutput, calls=%fused_computation.43 | convolution fusion | flops 8592031744 | bytes 20971520 | tf_op jit(solution)/shard_map/acnf,ang->cfg/dot_general | solution.py:135
  757.9 11.0 %bitcast_multiply_fusion = f32[2048,1024]{1,0:T(8,128)} fusion(bf16[2048,4,512]{2,0,1:T(8,128)(2,1)S(1)} %bitcast.127, bf16[4,512,1024]{2,1,0:T(8,128)(2,1)S(1)} %copy-done.4), kind=kOutput, calls=%fused_computation.42 | convolution fusion | flops 8592031744 | bytes 20971520 | tf_op jit(solution)/shard_map/acnf,ang->cfg/dot_general | solution.py:138
  (76 shorter events, 1.4 us)
Async XLA Ops:
  7.2 86.1 %copy-start = (bf16[512,1024]{1,0:T(8,128)(2,1)S(1)}, bf16[512,1024]{1,0:T(8,128)(2,1)}, u32[]{:S(2)}) copy-start(bf16[512,1024]{1,0:T(8,128)(2,1)} %param.9) | copy-start | bytes 3145732
  7.2 86.1 %copy-start.3 = (s32[6]{0:T(128)S(1)}, s32[6]{0:T(128)}, u32[]{:S(2)}) copy-start(s32[6]{0:T(128)} %param.13) | copy-start | bytes 76
  7.2 86.0 %all-gather.9.cloned.1.call-start = ((), (), s32[]{:S(2)}) async-start(), calls=%async_computation.1 | async-start | bytes 5242880 | tf_op jit(solution)/shard_map/all_gather | solution.py:39
  9.6 165.0 %all-gather.7.cloned.1.call-start = ((), (), s32[]{:S(2)}) async-start(), calls=%async_computation | async-start | bytes 5242880 | tf_op jit(solution)/shard_map/all_gather | solution.py:40
  12.0 243.5 %all-gather.15.cloned.1.call-start = ((), (), s32[]{:S(2)}) async-start(), calls=%async_computation.4 | async-start | bytes 5242880 | tf_op jit(solution)/shard_map/all_gather | solution.py:105
  12.7 324.2 %all-gather.13.cloned.1.call-start = ((), (), s32[]{:S(2)}) async-start(), calls=%async_computation.3 | async-start | bytes 5242880 | tf_op jit(solution)/shard_map/all_gather | solution.py:104
  15.0 447.3 %all-gather.11.cloned.1.call-start = ((), (), s32[]{:S(2)}) async-start(), calls=%async_computation.2 | async-start | bytes 9437184 | tf_op jit(solution)/shard_map/all_gather | solution.py:122
  208.8 128.1 %copy-start.2 = (bf16[512,1024]{1,0:T(8,128)(2,1)S(1)}, bf16[512,1024]{1,0:T(8,128)(2,1)}, u32[]{:S(2)}) copy-start(bf16[512,1024]{1,0:T(8,128)(2,1)} %param.10) | copy-start | bytes 3145732
  212.0 375.6 %all-gather.17.cloned.1.call-start = ((), (), s32[]{:S(2)}) async-start(), calls=%async_computation.5 | async-start | bytes 9437184 | tf_op jit(solution)/shard_map/all_gather | solution.py:123
  352.7 390.6 %all-reduce.3.cloned.1.call-start = ((), (), s32[]{:S(2)}) async-start(), calls=%async_computation.6 | async-start | bytes 16777216 | tf_op jit(solution)/shard_map/psum | solution.py:13
  743.3 14.6 %copy-start.1 = (bf16[2,1024,4,512]{3,1,0,2:T(8,128)(2,1)S(1)}, bf16[2,1024,4,512]{3,1,0,2:T(8,128)(2,1)}, u32[]{:S(2)}) copy-start(bf16[2,1024,4,512]{3,1,0,2:T(8,128)(2,1)} %copy.67) | copy-start | bytes 25165828
  743.3 14.6 %copy-start.4 = (bf16[4,512,1024]{2,1,0:T(8,128)(2,1)S(1)}, bf16[4,512,1024]{2,1,0:T(8,128)(2,1)}, u32[]{:S(2)}) copy-start(bf16[4,512,1024]{2,1,0:T(8,128)(2,1)} %get-tuple-element.384) | copy-start | bytes 12582916
Sparse Core Ops, SparseCore 0:
  9.7 83.4 all-gather.8
  95.4 79.2 all-gather.6
  176.2 79.2 all-gather.14
  256.9 79.9 all-gather.12
  339.5 122.8 all-gather.10
  464.9 122.6 all-gather.16
  592.2 151.0 all-reduce.2
where the time goes:
time: 777 us; the launch traced here: 776 us
  waiting for transfers between devices  594 us (76%)
  matrix products  67.8 us (9%)
  local copies, waits for them, and re-layouts  56 us (7%)
  other arithmetic  22.4 us (3%)
  blocking collectives  15.2 us (2%)
  between operations  14.2 us (2%)
    psum x1, waiting for transfers between devices, spread(): return lax.psum(kept, axis)  128 us
    all_gather x1, waiting for transfers between devices, on_device(): lax.all_gather(value_grads[None], ('tokens', 'cols'), axis=0, tiled=True)  121 us
    all_gather x1, waiting for transfers between devices, on_device(): lax.all_gather(attended[None], ('tokens', 'cols'), axis=0, tiled=True)  109 us
    all_gather x1, waiting for transfers between devices, on_device(): lax.all_gather(key_in, 'tokens', axis=0, tiled=True)  78.1 us
    all_gather x1, waiting for transfers between devices, on_device(): query_rows = lax.all_gather(query_in, 'tokens', axis=0, tiled=True)  59.8 us
    all_gather x1, waiting for transfers between devices, on_device(): lax.all_gather(value_in, 'tokens', axis=0, tiled=True)  54.3 us
    all_gather x1, waiting for transfers between devices, on_device(): grad_rows = lax.all_gather(out_grads, 'tokens', axis=0, tiled=True)  42.4 us
    dot_general x4, matrix products, update(): jnp.einsum('hqk,khd->qhd', weights, value_rows, preferred_element_type=jn...  20.8 us
  transfers between devices with their start and end apart: 7, of which 7 were waited for; matrix products, arithmetic and copies ran while one was open for 15% of the time, Pallas kernels for 0%

commit v1 on v0

--- a/solution.py
+++ b/solution.py
@@ -101,8 +101,11 @@
     (weighted, partials), _ = lax.scan(value_step, value_init, block_ids)
     attended = weighted.reshape(tok_dev, row_width).astype(jnp.bfloat16)
     stats_all = lax.all_gather(log_total.T, "tokens", axis=0, tiled=True)
-    query_rows = lax.all_gather(query_in, "tokens", axis=0, tiled=True)
-    grad_rows = lax.all_gather(out_grads, "tokens", axis=0, tiled=True)
+    query_rows, grad_rows = jnp.split(
+        jax.lax.all_gather(jnp.concatenate([query_in, out_grads], 1), "tokens", axis=0, tiled=True),
+        [query_in.shape[1]],
+        axis=1,
+    )
     piece_rows = query_rows.shape[0]
     piece_pos = jnp.arange(piece_rows, dtype=jnp.int32)
 

time: 777 us -> 765 us (0.985)
  waiting for transfers between devices: 594 us -> 582 us
    all_gather x2 -> x1, waiting for transfers between devices: 102 us -> 99 us  [on_device(): jax.lax.all_gather(jnp.concatenate([query_in, out_grads], 1), 'tokens', a...]
  transfers between devices with their start and end apart: 7 -> 6, of which waited for: 7 -> 6; matrix products, arithmetic and copies ran while one was open for 15% -> 15% of each run, Pallas kernels for 0% -> 0%
where the time goes in v1:
time: 765 us; the launch traced here: 764 us
  waiting for transfers between devices  582 us (76%)
  matrix products  68.5 us (9%)
  local copies, waits for them, and re-layouts  54.7 us (7%)
  other arithmetic  23.8 us (3%)
  between operations  14.3 us (2%)
  blocking collectives  14.2 us (2%)
    psum x1, waiting for transfers between devices, spread(): return lax.psum(kept, axis)  128 us
    all_gather x1, waiting for transfers between devices, on_device(): lax.all_gather(value_grads[None], ('tokens', 'cols'), axis=0, tiled=True)  121 us
    all_gather x1, waiting for transfers between devices, on_device(): lax.all_gather(attended[None], ('tokens', 'cols'), axis=0, tiled=True)  102 us
    all_gather x1, waiting for transfers between devices, on_device(): jax.lax.all_gather(jnp.concatenate([query_in, out_grads], 1), 'tokens', a...  99 us
    all_gather x1, waiting for transfers between devices, on_device(): lax.all_gather(key_in, 'tokens', axis=0, tiled=True)  78.5 us
    all_gather x1, waiting for transfers between devices, on_device(): lax.all_gather(value_in, 'tokens', axis=0, tiled=True)  53.7 us
    dot_general x4, matrix products, update(): jnp.einsum('hqk,khd->qhd', weights, value_rows, preferred_element_type=jn...  21 us
  transfers between devices with their start and end apart: 6, of which 6 were waited for; matrix products, arithmetic and copies ran while one was open for 15% of the time, Pallas kernels for 0%

profile of v1, /device:TPU:0, one launch (start us, length us, event | category | flops | bytes accessed | tf_op | source)
XLA Modules:
  0.0 763.5 jit_solution(1116125908499573518)
XLA Ops:
  7.2 2.4 copy.58
  9.7 2.3 copy.57
  12.1 0.5 copy.63
  12.7 0.5 copy.62
  13.2 1.5 pad_maximum_fusion
  14.8 78.5 %all-gather.8.cloned.1.call-done = bf16[2048,1024]{0,1:T(8,128)(2,1)} async-done(((bf16[512,1024]{0,1:T(8,128)(2,1)}), bf16[2048,1024]{0,1:T(8,128)(2,1)}) %all-gather.8.cloned.1.call-update) | async-done | bytes 4194320 | tf_op jit(solution)/shard_map/all_gather | solution.py:39
  93.3 27.1 %while.30 = (s32[]{:T(128)}, f32[8,512]{1,0:T(8,128)S(1)}, f32[8,512]{1,0:T(8,128)S(1)}, s32[6]{0:T(128)S(1)}, s32[4]{0:T(128)S(1)}, /*index=5*/bf16[2048,1024]{...) while((s32[]{:T(128)}, f32[8,512]{1,0:T(8,128)S(1)}, ...), condition=%wide.region_5.6_spmd.clone, body=%wide.region_0.5_spmd.clone.sunk | while | flops 553950208 | bytes 21995748 | solution.py:75
  93.3 0.6 dynamic_slice.60
  94.7 0.2 broadcast_compare_fusion.5
  94.9 1.3 constant_dynamic-slice_fusion.5
  96.2 1.7 fusion.60
  98.0 2.0 select_reduce_fusion.2
  100.1 0.6 dynamic_slice.60
  101.5 0.2 broadcast_compare_fusion.5
  101.7 1.3 constant_dynamic-slice_fusion.5
  103.0 1.7 fusion.60
  104.8 2.0 select_reduce_fusion.2
  106.9 0.6 dynamic_slice.60
  108.3 0.2 broadcast_compare_fusion.5
  108.5 1.3 constant_dynamic-slice_fusion.5
  109.8 1.7 fusion.60
  111.6 2.0 select_reduce_fusion.2
  113.7 0.6 dynamic_slice.60
  115.1 0.2 broadcast_compare_fusion.5
  115.3 1.3 constant_dynamic-slice_fusion.5
  116.6 1.7 fusion.60
  118.3 2.0 select_reduce_fusion.2
  120.4 53.7 %all-gather.6.cloned.1.call-done = bf16[2048,1024]{0,1:T(8,128)(2,1)} async-done(((bf16[512,1024]{0,1:T(8,128)(2,1)}), bf16[2048,1024]{0,1:T(8,128)(2,1)}) %all-gather.6.cloned.1.call-update) | async-done | bytes 4194320 | tf_op jit(solution)/shard_map/all_gather | solution.py:40
  174.1 34.0 %while.31 = (s32[]{:T(128)}, f32[512,8,128]{0,2,1:T(8,128)}, s32[4]{0:T(128)S(1)}, bf16[2048,1024]{0,1:T(8,128)(2,1)}, s32[6]{0:T(128)S(1)}, /*index=5*/bf16[204...) while((s32[]{:T(128)}, f32[512,8,128]{0,2,1:T(8,128)}, ...), condition=%wide.region_9.10_spmd.clone, body=%wide.region_6.9_spmd.clone.sunk | while | flops 1083460608 | bytes 12099821 | solution.py:101
  174.1 0.6 dynamic_slice.62
  175.4 0.2 broadcast_compare_fusion.6
  175.6 1.7 constant_dynamic-slice_fusion.6
  177.3 4.0 bitcast_add_fusion.2
  181.3 0.6 dynamic_slice.62
  182.5 0.2 broadcast_compare_fusion.6
  182.8 2.1 constant_dynamic-slice_fusion.6
  184.8 5.7 bitcast_add_fusion.2
  190.5 0.6 dynamic_slice.62
  191.8 0.2 broadcast_compare_fusion.6
  192.0 1.7 constant_dynamic-slice_fusion.6
  193.7 5.6 bitcast_add_fusion.2
  199.3 0.6 dynamic_slice.62
  200.6 0.2 broadcast_compare_fusion.6
  200.8 1.7 constant_dynamic-slice_fusion.6
  202.5 5.6 bitcast_add_fusion.2
  208.1 1.7 convert_element_type.76
  209.8 1.3 copy.73
  211.2 0.1 convert_reduce_fusion.4
  211.4 0.8 broadcast_compare_fusion.2
  212.2 14.2 %all_gather.22 = f32[2048,8]{0,1:T(8,128)S(1)} all-gather(f32[512,8]{0,1:T(8,128)S(1)} %bitcast.133), channel_id=1, replica_groups=mesh['heads'=4,'tokens'=4,'cols'=2] {'tokens'}, dimensions={0}, use_global_device_ids=true | all-gather | bytes 81920 | tf_op jit(solution)/shard_map/all_gather | solution.py:103
  226.4 99.0 %all-gather.12.cloned.1.call-done = bf16[2048,2048]{0,1:T(8,128)(2,1)} async-done(((bf16[512,2048]{0,1:T(8,128)(2,1)}), bf16[2048,2048]{0,1:T(8,128)(2,1)}) %all-gather.12.cloned.1.call-update) | async-done | bytes 8388624 | tf_op jit(solution)/shard_map/all_gather | solution.py:105
  325.4 6.1 fusion.36
  331.6 14.9 %fusion.29 = bf16[8,128,512]{2,1,0:T(8,128)(2,1)S(1)} fusion(bf16[2048,8,128]{0,2,1:T(8,128)(2,1)} %bitcast.131, bf16[2048,8,128]{0,2,1:T(8,128)(2,1)} %bitcast.130, f32[8,2048]{1,0:T(8,128)S(1)} %bitcast.134, pred[2048,512]{1,0:T(8,128)(4,1)S(1)} %broadcast_compare_fusion.2, bf16[512,1024]{1,0:T(8,128)(2,1)S(1)} %copy-done.3), kind=kOutput, calls=%fused_computation.51 | convolution fusion | flops 4329046016 | bytes 11599872 | tf_op jit(solution)/shard_map/hqk,qhd->khd/dot_general | solution.py:118
  346.4 1.3 copy.66
  347.8 0.3 all-reduce.3.cloned.1.call-start
  348.1 102.0 %all-gather.10.cloned.1.call-done = bf16[8,512,1024]{2,1,0:T(8,128)(2,1)} async-done(((bf16[1,512,1024]{2,1,0:T(8,128)(2,1)}), bf16[8,512,1024]{2,1,0:T(8,128)(2,1)}) %all-gather.10.cloned.1.call-update) | async-done | bytes 8388624 | tf_op jit(solution)/shard_map/all_gather | solution.py:125
  450.1 4.5 fusion.27
  454.6 120.8 %all-gather.14.cloned.1.call-done = bf16[8,512,1024]{2,1,0:T(8,128)(2,1)} async-done(((bf16[1,512,1024]{2,1,0:T(8,128)(2,1)}), bf16[8,512,1024]{2,1,0:T(8,128)(2,1)}) %all-gather.14.cloned.1.call-update) | async-done | bytes 8388624 | tf_op jit(solution)/shard_map/all_gather | solution.py:126
  575.3 4.4 fusion.26
  579.8 11.5 %copy.60 = bf16[2,1024,4,512]{3,1,0,2:T(8,128)(2,1)} copy(bf16[2,1024,4,512]{1,3,0,2:T(8,128)(2,1)} %bitcast.124) | data formatting | bytes 16777216 | tf_op jit(solution)/shard_map/acnf,ang->cfg/dot_general | solution.py:138
  591.3 11.5 %copy.67 = bf16[2,1024,4,512]{3,1,0,2:T(8,128)(2,1)} copy(bf16[2,1024,4,512]{1,3,0,2:T(8,128)(2,1)} %bitcast.126) | data formatting | bytes 16777216 | tf_op jit(solution)/shard_map/acnf,ang->cfg/dot_general | solution.py:141
  602.8 128.3 %all-reduce.3.cloned.1.call-done = (bf16[4,512,1024]{2,1,0:T(8,128)(2,1)}, bf16[4,512,1024]{2,1,0:T(8,128)(2,1)}) async-done(((bf16[4,512,1024]{2,1,0:T(8,128)(2,1)}, bf16[4,512,1024]{2,1,0:T(8,128)(2,1)}), (bf16[4,512,1024]{2,1,0:T(8,128)(2,1)}, bf16[4,512,1024]{2,1,0:T(8,128)(2,1)})) %all-reduce.3.cloned.1.call-update) | async-done | bytes 8388624 | tf_op jit(solution)/shard_map/psum | solution.py:13
  731.0 14.6 %bitcast_multiply_fusion.1 = f32[2048,1024]{1,0:T(8,128)} fusion(bf16[2048,4,512]{2,0,1:T(8,128)(2,1)} %bitcast.128, bf16[4,512,1024]{2,1,0:T(8,128)(2,1)} %get-tuple-element.383), kind=kOutput, calls=%fused_computation.43 | convolution fusion | flops 8592031744 | bytes 20971520 | tf_op jit(solution)/shard_map/acnf,ang->cfg/dot_general | solution.py:138
  745.6 11.0 %bitcast_multiply_fusion = f32[2048,1024]{1,0:T(8,128)} fusion(bf16[2048,4,512]{2,0,1:T(8,128)(2,1)S(1)} %bitcast.127, bf16[4,512,1024]{2,1,0:T(8,128)(2,1)S(1)} %copy-done.5), kind=kOutput, calls=%fused_computation.42 | convolution fusion | flops 8592031744 | bytes 20971520 | tf_op jit(solution)/shard_map/acnf,ang->cfg/dot_general | solution.py:141
  (77 shorter events, 1.4 us)
Async XLA Ops:
  7.2 4.9 copy-start.2
  7.2 5.5 copy-start
  7.2 86.1 %all-gather.8.cloned.1.call-start = ((), (), s32[]{:S(2)}) async-start(), calls=%async_computation.1 | async-start | bytes 5242880 | tf_op jit(solution)/shard_map/all_gather | solution.py:39
  9.7 164.4 %all-gather.6.cloned.1.call-start = ((), (), s32[]{:S(2)}) async-start(), calls=%async_computation | async-start | bytes 5242880 | tf_op jit(solution)/shard_map/all_gather | solution.py:40
  12.0 313.4 %all-gather.12.cloned.1.call-start = ((), (), s32[]{:S(2)}) async-start(), calls=%async_computation.3 | async-start | bytes 10485760 | tf_op jit(solution)/shard_map/all_gather | solution.py:105
  12.7 80.6 %copy-start.4 = (s32[6]{0:T(128)S(1)}, s32[6]{0:T(128)}, u32[]{:S(2)}) copy-start(s32[6]{0:T(128)} %param.13) | copy-start | bytes 76
  14.7 435.4 %all-gather.10.cloned.1.call-start = ((), (), s32[]{:S(2)}) async-start(), calls=%async_computation.2 | async-start | bytes 9437184 | tf_op jit(solution)/shard_map/all_gather | solution.py:125
  211.2 364.2 %all-gather.14.cloned.1.call-start = ((), (), s32[]{:S(2)}) async-start(), calls=%async_computation.4 | async-start | bytes 9437184 | tf_op jit(solution)/shard_map/all_gather | solution.py:126
  226.4 105.2 %copy-start.3 = (bf16[512,1024]{1,0:T(8,128)(2,1)S(1)}, bf16[512,1024]{1,0:T(8,128)(2,1)}, u32[]{:S(2)}) copy-start(bf16[512,1024]{1,0:T(8,128)(2,1)} %param.10) | copy-start | bytes 3145732
  347.8 383.2 %all-reduce.3.cloned.1.call-start = ((), (), s32[]{:S(2)}) async-start(), calls=%async_computation.5 | async-start | bytes 16777216 | tf_op jit(solution)/shard_map/psum | solution.py:13
  731.0 14.6 %copy-start.1 = (bf16[2,1024,4,512]{3,1,0,2:T(8,128)(2,1)S(1)}, bf16[2,1024,4,512]{3,1,0,2:T(8,128)(2,1)}, u32[]{:S(2)}) copy-start(bf16[2,1024,4,512]{3,1,0,2:T(8,128)(2,1)} %copy.67) | copy-start | bytes 25165828
  731.0 14.6 %copy-start.5 = (bf16[4,512,1024]{2,1,0:T(8,128)(2,1)S(1)}, bf16[4,512,1024]{2,1,0:T(8,128)(2,1)}, u32[]{:S(2)}) copy-start(bf16[4,512,1024]{2,1,0:T(8,128)(2,1)} %get-tuple-element.384) | copy-start | bytes 12582916
Sparse Core Ops, SparseCore 0:
  9.8 83.4 all-gather.7
  94.9 79.2 all-gather.5
  176.3 149.0 all-gather.11
  327.4 122.6 all-gather.9
  452.7 122.6 all-gather.13
  579.9 151.0 all-reduce.2
